TPU v7x, 32 devices: a whole 2x2x4 slice. The times are simulated.
32 devices in a mesh: ctx: 4 (over z), head: 4 (over y, x), grp: 2 (over core).
Axes of the slice: x: 2, y: 2, z: 4, core: 2. Of those that a mesh axis runs over, the one named last changes fastest.
Arguments:
- prompt_queries: bfloat16 [4096, 8192], P(('ctx', 'grp'), 'head'), may hold values from -16 to 16
- rotated_prompt_keys: bfloat16 [4096, 1024], P(('ctx', 'grp'), 'head'), may hold values from -12 to 12
- prompt_value_rows: bfloat16 [4096, 1024], P(('ctx', 'grp'), 'head'), may hold values from -12 to 12
- continuation_queries: bfloat16 [384, 8192], P(('ctx', 'grp'), 'head'), may hold values from -16 to 16
- prefix_len: int32 [384], replicated, may hold values from 2 to 4096
- out_weight: bfloat16 [8192, 8192], P('head', ('ctx', 'grp')), may hold values from -0.0625 to 0.0625
Outputs:
- prompt_context: bfloat16 [4096, 8192], P(('ctx', 'grp'), 'head')
- mixed: bfloat16 [384, 8192], P('head', ('ctx', 'grp'))
Inputs may be any that keep to these rules, and one draw needn't show every extreme that they name: Continuation b reads prompt positions 0 to prefix_len[b] - 1.
All inputs are finite; a program needn't handle non-finite values.
Results may differ from a plain program's by a relative error of at most 0.018.
Values may be sent and summed in bfloat16 or wider, within the bound.
No kernel may reach another device: no remote copies, remote signals or barrier semaphores. Data moves between devices by JAX's collectives and lax.ppermute only.
A program may use at most 128 MiB of HBM per device.

v0:
```python
import jax
import jax.numpy as jnp
from jax import lax
from jax.sharding import PartitionSpec as P

QUERY_HEADS = 64
KEY_VALUE_HEADS = 8
HEAD_WIDTH = 128


NEG = -1e30


def empty_state(row_count, heads_kv, query_group_count):
    return (
        jnp.full((row_count, heads_kv, query_group_count), NEG, jnp.float32),
        jnp.zeros((row_count, heads_kv, query_group_count), jnp.float32),
        jnp.zeros((row_count, heads_kv, query_group_count, HEAD_WIDTH), jnp.float32),
    )


def attend(state_now, queries, allowed, key_rows, value_rows):
    maxima, totals, weighted = state_now
    heads_kv = weighted.shape[1]
    expanded_key_heads = key_rows.reshape(key_rows.shape[0], heads_kv, HEAD_WIDTH)
    expanded_value_heads = value_rows.reshape(value_rows.shape[0], heads_kv, HEAD_WIDTH)
    scores = jnp.einsum(
        "rkgd,nkd->rkgn", queries, expanded_key_heads, preferred_element_type=jnp.float32
    ) * HEAD_WIDTH ** (-0.5)
    scores = jnp.where(allowed[:, None, None, :], scores, NEG)
    raised = jnp.maximum(maxima, jnp.max(scores, axis=3))
    factor = jnp.exp(maxima - raised)
    powers = jnp.exp(scores - raised[..., None])
    totals = totals * factor + jnp.sum(powers, axis=3)
    weighted = weighted * factor[..., None] + jnp.einsum(
        "rkgn,nkd->rkgd",
        powers.astype(jnp.bfloat16),
        expanded_value_heads,
        preferred_element_type=jnp.float32,
    )
    return (raised, totals, weighted)


def prompt_step(state_now, queries, places, prefix_piece, first_row):
    key_rows, value_rows = prefix_piece
    key_places = first_row + jnp.arange(key_rows.shape[0], dtype=jnp.int32)
    allowed = key_places[None, :] <= places[:, None]
    return lax.cond(
        first_row <= places[-1],
        lambda state_in: attend(state_in, queries, allowed, key_rows, value_rows),
        lambda state_in: state_in,
        state_now,
    )


def finish(state_now):
    maxima, totals, weighted = state_now
    context = (weighted / totals[..., None]).astype(jnp.bfloat16)
    return context.reshape(context.shape[0], -1)


def local_fold(advance, initial, prefix_pair, block_rows):
    key_all, value_all = prefix_pair
    block_count = key_all.shape[0] // block_rows

    def visit(number, state_now):
        first_row = number * block_rows
        prefix_piece = (
            lax.dynamic_slice_in_dim(key_all, first_row, block_rows, 0),
            lax.dynamic_slice_in_dim(value_all, first_row, block_rows, 0),
        )
        return advance(state_now, prefix_piece, first_row)

    return lax.fori_loop(0, block_count, visit, initial)


def local(
    prompt_queries,
    rotated_prompt_keys,
    prompt_value_rows,
    continuation_queries,
    prefix_len,
    out_weight,
):
    my_index = lax.axis_index(("ctx", "grp"))
    block_rows = prompt_queries.shape[0]
    heads_kv = rotated_prompt_keys.shape[1] // HEAD_WIDTH
    query_group_count = QUERY_HEADS // KEY_VALUE_HEADS
    gathered_prefix = (
        lax.all_gather(rotated_prompt_keys, ("ctx", "grp"), axis=0, tiled=True),
        lax.all_gather(prompt_value_rows, ("ctx", "grp"), axis=0, tiled=True),
    )

    def sweep_prefix(advance, initial):
        return local_fold(advance, initial, gathered_prefix, block_rows)

    places = my_index * block_rows + jnp.arange(block_rows, dtype=jnp.int32)
    queries = prompt_queries.reshape(block_rows, heads_kv, query_group_count, HEAD_WIDTH)

    def prompt_fold(state_now, prefix_piece, first_row):
        return prompt_step(state_now, queries, places, prefix_piece, first_row)

    prompt_context = finish(
        sweep_prefix(prompt_fold, empty_state(block_rows, heads_kv, query_group_count))
    )
    own_rows = continuation_queries.shape[0]
    lengths_own = lax.dynamic_slice_in_dim(prefix_len, my_index * own_rows, own_rows, 0)
    decode_heads = continuation_queries.reshape(own_rows, heads_kv, query_group_count, HEAD_WIDTH)

    def decode_fold(state_now, prefix_piece, first_row):
        key_rows, value_rows = prefix_piece
        key_places = first_row + jnp.arange(key_rows.shape[0], dtype=jnp.int32)
        allowed = key_places[None, :] < lengths_own[:, None]
        return attend(state_now, decode_heads, allowed, key_rows, value_rows)

    continuation_context = finish(
        sweep_prefix(decode_fold, empty_state(own_rows, heads_kv, query_group_count))
    )
    gathered = lax.all_gather(continuation_context, ("ctx", "grp"), axis=0, tiled=True)
    mixed = lax.psum_scatter(
        jnp.dot(gathered, out_weight, preferred_element_type=jnp.float32).astype(jnp.bfloat16),
        "head",
        scatter_dimension=0,
        tiled=True,
    )
    return (prompt_context, mixed)


def solution(mesh):
    in_specs = (
        P(("ctx", "grp"), "head"),
        P(("ctx", "grp"), "head"),
        P(("ctx", "grp"), "head"),
        P(("ctx", "grp"), "head"),
        P(),
        P("head", ("ctx", "grp")),
    )
    out_specs = (P(("ctx", "grp"), "head"), P("head", ("ctx", "grp")))
    return jax.shard_map(local, mesh=mesh, in_specs=in_specs, out_specs=out_specs, check_vma=False)
```

profile of v0, /device:TPU:25, one launch (start us, length us, event | category | flops | bytes accessed | tf_op | source)
XLA Modules:
  0.0 384.7 jit_solution(5373572100884947731)
XLA Ops:
  7.2 1.8 copy.15
  9.1 1.8 copy.17
  12.8 26.4 %all-gather.4.cloned.1.call-done = bf16[4096,256]{0,1:T(8,128)(2,1)} async-done(((bf16[512,256]{0,1:T(8,128)(2,1)}), bf16[4096,256]{0,1:T(8,128)(2,1)}) %all-gather.4.cloned.1.call-update) | async-done | bytes 2097168 | tf_op jit(solution)/shard_map/all_gather | solution.py:90
  39.2 30.2 %all-gather.6.cloned.1.call-done = bf16[4096,256]{0,1:T(8,128)(2,1)} async-done(((bf16[512,256]{0,1:T(8,128)(2,1)}), bf16[4096,256]{0,1:T(8,128)(2,1)}) %all-gather.6.cloned.1.call-update) | async-done | bytes 2097168 | tf_op jit(solution)/shard_map/all_gather | solution.py:91
  69.4 21.9 %while.36 = (s32[]{:T(128)}, f32[48,2,8]{0,2,1:T(8,128)S(1)}, f32[48,2,8]{0,2,1:T(8,128)S(1)}, f32[48,2,8,128]{3,0,2,1:T(8,128)S(1)}, s32[48]{0:T(128)S(1)}, /*i...) while((s32[]{:T(128)}, f32[48,2,8]{0,2,1:T(8,128)S(1)}, ...), condition=%wide.region_9.10_spmd.clone, body=%wide.region_6.9_spmd.clone.sunk | while | flops 204402944 | bytes 7377279 | solution.py:74
  72.1 1.1 constant_dynamic-slice_fusion.5
  92.3 24.5 %all-gather.8.cloned.1.call-done = bf16[384,2048]{1,0:T(8,128)(2,1)} async-done(((bf16[48,2048]{1,0:T(8,128)(2,1)}), bf16[384,2048]{1,0:T(8,128)(2,1)}) %all-gather.8.cloned.1.call-update) | async-done | bytes 1572880 | tf_op jit(solution)/shard_map/all_gather | solution.py:119
  116.8 5.4 %convolution_convert_fusion = bf16[384,1024]{1,0:T(8,128)(2,1)} fusion(bf16[384,2048]{1,0:T(8,128)(2,1)} %all-gather.8.cloned.1.call-done, bf16[2048,1024]{1,0:T(8,128)(2,1)} %param.17), kind=kOutput, calls=%fused_computation.34 | convolution fusion | flops 1611005952 | bytes 6553600 | tf_op jit(solution)/shard_map/dot_general | solution.py:121
  122.2 2.7 copy.16
  124.9 3.0 copy.18
  128.0 2.4 broadcast_in_dim.90
  130.4 241.7 %while.35 = (s32[]{:T(128)}, f32[512,2,8]{0,2,1:T(8,128)S(1)}, f32[512,2,8]{0,2,1:T(8,128)S(1)}, f32[512,2,8,128]{3,0,2,1:T(8,128)}, s32[512]{0:T(512)S(1)}, /*i...) while((s32[]{:T(128)}, f32[512,2,8]{0,2,1:T(8,128)S(1)}, ...), condition=%wide.region_5.6_spmd, body=%wide.region_0.5_spmd.sunk | while | flops 2195997184 | bytes 63973688 | solution.py:74
  131.6 29.1 %conditional.2 = ((f32[512,2,8]{0,2,1:T(8,128)S(1)}, f32[512,2,8]{0,2,1:T(8,128)S(1)}, f32[512,2,8,128]{3,0,2,1:T(8,128)})) conditional(s32[]{:T(128)} %convert_element_type.44, (f32[512,2,8]{0,2,1:T(8,128)S(1)}, f32[512,2,8]{0,2,1:T(8,128)S(1)}, f32[512,2,8,128]{3,0,2,1:T(8,128)}) %tuple.87, (s32[]{:T(128)}, s32[1,512]{1,0:T(1,128)S(1)}, ...), branch_computations={%region_1.0_spmd, %region_2.4_spmd} | conditional | flops 2195997184 | bytes 63971400 | solution.py:48
  131.9 1.1 constant_dynamic-slice_fusion
  133.0 7.5 %fusion.2 = (f32[512,2,8]{0,2,1:T(8,128)S(1)}, f32[2,512,512,8]{2,1,3,0:T(8,128)}) fusion(pred[512,512]{0,1:T(8,128)(4,1)S(1)} %broadcast_compare_fusion, bf16[512,2,128,1]{0,2,3,1:T(8,128)(2,1)S(1)} %bitcast.77, bf16[512,2,8,128]{3,0,2,1:T(8,128)(2,1)S(1)} %get-tuple-element.379), kind=kOutput, calls=%fused_computation.4 | convolution fusion | flops 1086316544 | bytes 19431424 | tf_op jit(solution)/shard_map/while/body/eval_jaxpr/cond/branch_1_fun/rkgd,nkd->rkgn/dot_general | solution.py:27
  140.5 9.3 %fusion.1 = f32[512,2,8]{0,2,1:T(8,128)S(1)} fusion(f32[2,512,512,8]{2,1,3,0:T(8,128)} %get-tuple-element.494, f32[512,2,8]{0,2,1:T(8,128)S(1)} %max.11, pred[512,512]{0,1:T(8,128)(4,1)S(1)} %broadcast_compare_fusion), kind=kLoop, calls=%fused_computation.3 | loop fusion | flops 16769024 | bytes 17104896 | tf_op jit(solution)/shard_map/while/body/eval_jaxpr/cond/branch_1_fun/reduce_sum | solution.py:34
  149.8 10.9 %bitcast_add_fusion = f32[512,2,8,128]{3,0,2,1:T(8,128)} fusion(f32[512,2,8,128]{3,0,2,1:T(8,128)} %get-tuple-element.381, bf16[512,2,128,1]{0,2,3,1:T(8,128)(2,1)S(1)} %bitcast.82, f32[2,512,512,8]{2,1,3,0:T(8,128)} %get-tuple-element.494, f32[512,2,8]{0,2,1:T(8,128)S(1)} %max.11, pred[512,512]{0,1:T(8,128)(4,1)S(1)} %broadcast_compare_fusion, ...), kind=kOutput, calls=%fused_computation.7 | convolution fusion | flops 1092616192 | bytes 25755648 | tf_op jit(solution)/shard_map/while/body/eval_jaxpr/cond/branch_1_fun/rkgn,nkd->rkgd/dot_general | solution.py:35
  162.0 28.9 %conditional.2 = ((f32[512,2,8]{0,2,1:T(8,128)S(1)}, f32[512,2,8]{0,2,1:T(8,128)S(1)}, f32[512,2,8,128]{3,0,2,1:T(8,128)})) conditional(s32[]{:T(128)} %convert_element_type.44, (f32[512,2,8]{0,2,1:T(8,128)S(1)}, f32[512,2,8]{0,2,1:T(8,128)S(1)}, f32[512,2,8,128]{3,0,2,1:T(8,128)}) %tuple.87, (s32[]{:T(128)}, s32[1,512]{1,0:T(1,128)S(1)}, ...), branch_computations={%region_1.0_spmd, %region_2.4_spmd} | conditional | flops 2195997184 | bytes 63971400 | solution.py:48
  163.4 7.4 %fusion.2 = (f32[512,2,8]{0,2,1:T(8,128)S(1)}, f32[2,512,512,8]{2,1,3,0:T(8,128)}) fusion(pred[512,512]{0,1:T(8,128)(4,1)S(1)} %broadcast_compare_fusion, bf16[512,2,128,1]{0,2,3,1:T(8,128)(2,1)S(1)} %bitcast.77, bf16[512,2,8,128]{3,0,2,1:T(8,128)(2,1)S(1)} %get-tuple-element.379), kind=kOutput, calls=%fused_computation.4 | convolution fusion | flops 1086316544 | bytes 19431424 | tf_op jit(solution)/shard_map/while/body/eval_jaxpr/cond/branch_1_fun/rkgd,nkd->rkgn/dot_general | solution.py:27
  170.8 9.2 %fusion.1 = f32[512,2,8]{0,2,1:T(8,128)S(1)} fusion(f32[2,512,512,8]{2,1,3,0:T(8,128)} %get-tuple-element.494, f32[512,2,8]{0,2,1:T(8,128)S(1)} %max.11, pred[512,512]{0,1:T(8,128)(4,1)S(1)} %broadcast_compare_fusion), kind=kLoop, calls=%fused_computation.3 | loop fusion | flops 16769024 | bytes 17104896 | tf_op jit(solution)/shard_map/while/body/eval_jaxpr/cond/branch_1_fun/reduce_sum | solution.py:34
  180.0 10.9 %bitcast_add_fusion = f32[512,2,8,128]{3,0,2,1:T(8,128)} fusion(f32[512,2,8,128]{3,0,2,1:T(8,128)} %get-tuple-element.381, bf16[512,2,128,1]{0,2,3,1:T(8,128)(2,1)S(1)} %bitcast.82, f32[2,512,512,8]{2,1,3,0:T(8,128)} %get-tuple-element.494, f32[512,2,8]{0,2,1:T(8,128)S(1)} %max.11, pred[512,512]{0,1:T(8,128)(4,1)S(1)} %broadcast_compare_fusion, ...), kind=kOutput, calls=%fused_computation.7 | convolution fusion | flops 1092616192 | bytes 25755648 | tf_op jit(solution)/shard_map/while/body/eval_jaxpr/cond/branch_1_fun/rkgn,nkd->rkgd/dot_general | solution.py:35
  192.2 28.9 %conditional.2 = ((f32[512,2,8]{0,2,1:T(8,128)S(1)}, f32[512,2,8]{0,2,1:T(8,128)S(1)}, f32[512,2,8,128]{3,0,2,1:T(8,128)})) conditional(s32[]{:T(128)} %convert_element_type.44, (f32[512,2,8]{0,2,1:T(8,128)S(1)}, f32[512,2,8]{0,2,1:T(8,128)S(1)}, f32[512,2,8,128]{3,0,2,1:T(8,128)}) %tuple.87, (s32[]{:T(128)}, s32[1,512]{1,0:T(1,128)S(1)}, ...), branch_computations={%region_1.0_spmd, %region_2.4_spmd} | conditional | flops 2195997184 | bytes 63971400 | solution.py:48
  193.6 7.4 %fusion.2 = (f32[512,2,8]{0,2,1:T(8,128)S(1)}, f32[2,512,512,8]{2,1,3,0:T(8,128)}) fusion(pred[512,512]{0,1:T(8,128)(4,1)S(1)} %broadcast_compare_fusion, bf16[512,2,128,1]{0,2,3,1:T(8,128)(2,1)S(1)} %bitcast.77, bf16[512,2,8,128]{3,0,2,1:T(8,128)(2,1)S(1)} %get-tuple-element.379), kind=kOutput, calls=%fused_computation.4 | convolution fusion | flops 1086316544 | bytes 19431424 | tf_op jit(solution)/shard_map/while/body/eval_jaxpr/cond/branch_1_fun/rkgd,nkd->rkgn/dot_general | solution.py:27
  201.0 9.2 %fusion.1 = f32[512,2,8]{0,2,1:T(8,128)S(1)} fusion(f32[2,512,512,8]{2,1,3,0:T(8,128)} %get-tuple-element.494, f32[512,2,8]{0,2,1:T(8,128)S(1)} %max.11, pred[512,512]{0,1:T(8,128)(4,1)S(1)} %broadcast_compare_fusion), kind=kLoop, calls=%fused_computation.3 | loop fusion | flops 16769024 | bytes 17104896 | tf_op jit(solution)/shard_map/while/body/eval_jaxpr/cond/branch_1_fun/reduce_sum | solution.py:34
  210.2 10.9 %bitcast_add_fusion = f32[512,2,8,128]{3,0,2,1:T(8,128)} fusion(f32[512,2,8,128]{3,0,2,1:T(8,128)} %get-tuple-element.381, bf16[512,2,128,1]{0,2,3,1:T(8,128)(2,1)S(1)} %bitcast.82, f32[2,512,512,8]{2,1,3,0:T(8,128)} %get-tuple-element.494, f32[512,2,8]{0,2,1:T(8,128)S(1)} %max.11, pred[512,512]{0,1:T(8,128)(4,1)S(1)} %broadcast_compare_fusion, ...), kind=kOutput, calls=%fused_computation.7 | convolution fusion | flops 1092616192 | bytes 25755648 | tf_op jit(solution)/shard_map/while/body/eval_jaxpr/cond/branch_1_fun/rkgn,nkd->rkgd/dot_general | solution.py:35
  222.4 28.9 %conditional.2 = ((f32[512,2,8]{0,2,1:T(8,128)S(1)}, f32[512,2,8]{0,2,1:T(8,128)S(1)}, f32[512,2,8,128]{3,0,2,1:T(8,128)})) conditional(s32[]{:T(128)} %convert_element_type.44, (f32[512,2,8]{0,2,1:T(8,128)S(1)}, f32[512,2,8]{0,2,1:T(8,128)S(1)}, f32[512,2,8,128]{3,0,2,1:T(8,128)}) %tuple.87, (s32[]{:T(128)}, s32[1,512]{1,0:T(1,128)S(1)}, ...), branch_computations={%region_1.0_spmd, %region_2.4_spmd} | conditional | flops 2195997184 | bytes 63971400 | solution.py:48
  223.7 7.4 %fusion.2 = (f32[512,2,8]{0,2,1:T(8,128)S(1)}, f32[2,512,512,8]{2,1,3,0:T(8,128)}) fusion(pred[512,512]{0,1:T(8,128)(4,1)S(1)} %broadcast_compare_fusion, bf16[512,2,128,1]{0,2,3,1:T(8,128)(2,1)S(1)} %bitcast.77, bf16[512,2,8,128]{3,0,2,1:T(8,128)(2,1)S(1)} %get-tuple-element.379), kind=kOutput, calls=%fused_computation.4 | convolution fusion | flops 1086316544 | bytes 19431424 | tf_op jit(solution)/shard_map/while/body/eval_jaxpr/cond/branch_1_fun/rkgd,nkd->rkgn/dot_general | solution.py:27
  231.2 9.2 %fusion.1 = f32[512,2,8]{0,2,1:T(8,128)S(1)} fusion(f32[2,512,512,8]{2,1,3,0:T(8,128)} %get-tuple-element.494, f32[512,2,8]{0,2,1:T(8,128)S(1)} %max.11, pred[512,512]{0,1:T(8,128)(4,1)S(1)} %broadcast_compare_fusion), kind=kLoop, calls=%fused_computation.3 | loop fusion | flops 16769024 | bytes 17104896 | tf_op jit(solution)/shard_map/while/body/eval_jaxpr/cond/branch_1_fun/reduce_sum | solution.py:34
  240.4 10.9 %bitcast_add_fusion = f32[512,2,8,128]{3,0,2,1:T(8,128)} fusion(f32[512,2,8,128]{3,0,2,1:T(8,128)} %get-tuple-element.381, bf16[512,2,128,1]{0,2,3,1:T(8,128)(2,1)S(1)} %bitcast.82, f32[2,512,512,8]{2,1,3,0:T(8,128)} %get-tuple-element.494, f32[512,2,8]{0,2,1:T(8,128)S(1)} %max.11, pred[512,512]{0,1:T(8,128)(4,1)S(1)} %broadcast_compare_fusion, ...), kind=kOutput, calls=%fused_computation.7 | convolution fusion | flops 1092616192 | bytes 25755648 | tf_op jit(solution)/shard_map/while/body/eval_jaxpr/cond/branch_1_fun/rkgn,nkd->rkgd/dot_general | solution.py:35
  252.6 28.9 %conditional.2 = ((f32[512,2,8]{0,2,1:T(8,128)S(1)}, f32[512,2,8]{0,2,1:T(8,128)S(1)}, f32[512,2,8,128]{3,0,2,1:T(8,128)})) conditional(s32[]{:T(128)} %convert_element_type.44, (f32[512,2,8]{0,2,1:T(8,128)S(1)}, f32[512,2,8]{0,2,1:T(8,128)S(1)}, f32[512,2,8,128]{3,0,2,1:T(8,128)}) %tuple.87, (s32[]{:T(128)}, s32[1,512]{1,0:T(1,128)S(1)}, ...), branch_computations={%region_1.0_spmd, %region_2.4_spmd} | conditional | flops 2195997184 | bytes 63971400 | solution.py:48
  253.9 7.4 %fusion.2 = (f32[512,2,8]{0,2,1:T(8,128)S(1)}, f32[2,512,512,8]{2,1,3,0:T(8,128)}) fusion(pred[512,512]{0,1:T(8,128)(4,1)S(1)} %broadcast_compare_fusion, bf16[512,2,128,1]{0,2,3,1:T(8,128)(2,1)S(1)} %bitcast.77, bf16[512,2,8,128]{3,0,2,1:T(8,128)(2,1)S(1)} %get-tuple-element.379), kind=kOutput, calls=%fused_computation.4 | convolution fusion | flops 1086316544 | bytes 19431424 | tf_op jit(solution)/shard_map/while/body/eval_jaxpr/cond/branch_1_fun/rkgd,nkd->rkgn/dot_general | solution.py:27
  261.4 9.2 %fusion.1 = f32[512,2,8]{0,2,1:T(8,128)S(1)} fusion(f32[2,512,512,8]{2,1,3,0:T(8,128)} %get-tuple-element.494, f32[512,2,8]{0,2,1:T(8,128)S(1)} %max.11, pred[512,512]{0,1:T(8,128)(4,1)S(1)} %broadcast_compare_fusion), kind=kLoop, calls=%fused_computation.3 | loop fusion | flops 16769024 | bytes 17104896 | tf_op jit(solution)/shard_map/while/body/eval_jaxpr/cond/branch_1_fun/reduce_sum | solution.py:34
  270.6 10.9 %bitcast_add_fusion = f32[512,2,8,128]{3,0,2,1:T(8,128)} fusion(f32[512,2,8,128]{3,0,2,1:T(8,128)} %get-tuple-element.381, bf16[512,2,128,1]{0,2,3,1:T(8,128)(2,1)S(1)} %bitcast.82, f32[2,512,512,8]{2,1,3,0:T(8,128)} %get-tuple-element.494, f32[512,2,8]{0,2,1:T(8,128)S(1)} %max.11, pred[512,512]{0,1:T(8,128)(4,1)S(1)} %broadcast_compare_fusion, ...), kind=kOutput, calls=%fused_computation.7 | convolution fusion | flops 1092616192 | bytes 25755648 | tf_op jit(solution)/shard_map/while/body/eval_jaxpr/cond/branch_1_fun/rkgn,nkd->rkgd/dot_general | solution.py:35
  282.8 28.9 %conditional.2 = ((f32[512,2,8]{0,2,1:T(8,128)S(1)}, f32[512,2,8]{0,2,1:T(8,128)S(1)}, f32[512,2,8,128]{3,0,2,1:T(8,128)})) conditional(s32[]{:T(128)} %convert_element_type.44, (f32[512,2,8]{0,2,1:T(8,128)S(1)}, f32[512,2,8]{0,2,1:T(8,128)S(1)}, f32[512,2,8,128]{3,0,2,1:T(8,128)}) %tuple.87, (s32[]{:T(128)}, s32[1,512]{1,0:T(1,128)S(1)}, ...), branch_computations={%region_1.0_spmd, %region_2.4_spmd} | conditional | flops 2195997184 | bytes 63971400 | solution.py:48
  284.1 7.4 %fusion.2 = (f32[512,2,8]{0,2,1:T(8,128)S(1)}, f32[2,512,512,8]{2,1,3,0:T(8,128)}) fusion(pred[512,512]{0,1:T(8,128)(4,1)S(1)} %broadcast_compare_fusion, bf16[512,2,128,1]{0,2,3,1:T(8,128)(2,1)S(1)} %bitcast.77, bf16[512,2,8,128]{3,0,2,1:T(8,128)(2,1)S(1)} %get-tuple-element.379), kind=kOutput, calls=%fused_computation.4 | convolution fusion | flops 1086316544 | bytes 19431424 | tf_op jit(solution)/shard_map/while/body/eval_jaxpr/cond/branch_1_fun/rkgd,nkd->rkgn/dot_general | solution.py:27
  291.6 9.2 %fusion.1 = f32[512,2,8]{0,2,1:T(8,128)S(1)} fusion(f32[2,512,512,8]{2,1,3,0:T(8,128)} %get-tuple-element.494, f32[512,2,8]{0,2,1:T(8,128)S(1)} %max.11, pred[512,512]{0,1:T(8,128)(4,1)S(1)} %broadcast_compare_fusion), kind=kLoop, calls=%fused_computation.3 | loop fusion | flops 16769024 | bytes 17104896 | tf_op jit(solution)/shard_map/while/body/eval_jaxpr/cond/branch_1_fun/reduce_sum | solution.py:34
  300.8 10.9 %bitcast_add_fusion = f32[512,2,8,128]{3,0,2,1:T(8,128)} fusion(f32[512,2,8,128]{3,0,2,1:T(8,128)} %get-tuple-element.381, bf16[512,2,128,1]{0,2,3,1:T(8,128)(2,1)S(1)} %bitcast.82, f32[2,512,512,8]{2,1,3,0:T(8,128)} %get-tuple-element.494, f32[512,2,8]{0,2,1:T(8,128)S(1)} %max.11, pred[512,512]{0,1:T(8,128)(4,1)S(1)} %broadcast_compare_fusion, ...), kind=kOutput, calls=%fused_computation.7 | convolution fusion | flops 1092616192 | bytes 25755648 | tf_op jit(solution)/shard_map/while/body/eval_jaxpr/cond/branch_1_fun/rkgn,nkd->rkgd/dot_general | solution.py:35
  313.0 28.9 %conditional.2 = ((f32[512,2,8]{0,2,1:T(8,128)S(1)}, f32[512,2,8]{0,2,1:T(8,128)S(1)}, f32[512,2,8,128]{3,0,2,1:T(8,128)})) conditional(s32[]{:T(128)} %convert_element_type.44, (f32[512,2,8]{0,2,1:T(8,128)S(1)}, f32[512,2,8]{0,2,1:T(8,128)S(1)}, f32[512,2,8,128]{3,0,2,1:T(8,128)}) %tuple.87, (s32[]{:T(128)}, s32[1,512]{1,0:T(1,128)S(1)}, ...), branch_computations={%region_1.0_spmd, %region_2.4_spmd} | conditional | flops 2195997184 | bytes 63971400 | solution.py:48
  314.3 7.4 %fusion.2 = (f32[512,2,8]{0,2,1:T(8,128)S(1)}, f32[2,512,512,8]{2,1,3,0:T(8,128)}) fusion(pred[512,512]{0,1:T(8,128)(4,1)S(1)} %broadcast_compare_fusion, bf16[512,2,128,1]{0,2,3,1:T(8,128)(2,1)S(1)} %bitcast.77, bf16[512,2,8,128]{3,0,2,1:T(8,128)(2,1)S(1)} %get-tuple-element.379), kind=kOutput, calls=%fused_computation.4 | convolution fusion | flops 1086316544 | bytes 19431424 | tf_op jit(solution)/shard_map/while/body/eval_jaxpr/cond/branch_1_fun/rkgd,nkd->rkgn/dot_general | solution.py:27
  321.7 9.2 %fusion.1 = f32[512,2,8]{0,2,1:T(8,128)S(1)} fusion(f32[2,512,512,8]{2,1,3,0:T(8,128)} %get-tuple-element.494, f32[512,2,8]{0,2,1:T(8,128)S(1)} %max.11, pred[512,512]{0,1:T(8,128)(4,1)S(1)} %broadcast_compare_fusion), kind=kLoop, calls=%fused_computation.3 | loop fusion | flops 16769024 | bytes 17104896 | tf_op jit(solution)/shard_map/while/body/eval_jaxpr/cond/branch_1_fun/reduce_sum | solution.py:34
  331.0 10.9 %bitcast_add_fusion = f32[512,2,8,128]{3,0,2,1:T(8,128)} fusion(f32[512,2,8,128]{3,0,2,1:T(8,128)} %get-tuple-element.381, bf16[512,2,128,1]{0,2,3,1:T(8,128)(2,1)S(1)} %bitcast.82, f32[2,512,512,8]{2,1,3,0:T(8,128)} %get-tuple-element.494, f32[512,2,8]{0,2,1:T(8,128)S(1)} %max.11, pred[512,512]{0,1:T(8,128)(4,1)S(1)} %broadcast_compare_fusion, ...), kind=kOutput, calls=%fused_computation.7 | convolution fusion | flops 1092616192 | bytes 25755648 | tf_op jit(solution)/shard_map/while/body/eval_jaxpr/cond/branch_1_fun/rkgn,nkd->rkgd/dot_general | solution.py:35
  343.2 28.9 %conditional.2 = ((f32[512,2,8]{0,2,1:T(8,128)S(1)}, f32[512,2,8]{0,2,1:T(8,128)S(1)}, f32[512,2,8,128]{3,0,2,1:T(8,128)})) conditional(s32[]{:T(128)} %convert_element_type.44, (f32[512,2,8]{0,2,1:T(8,128)S(1)}, f32[512,2,8]{0,2,1:T(8,128)S(1)}, f32[512,2,8,128]{3,0,2,1:T(8,128)}) %tuple.87, (s32[]{:T(128)}, s32[1,512]{1,0:T(1,128)S(1)}, ...), branch_computations={%region_1.0_spmd, %region_2.4_spmd} | conditional | flops 2195997184 | bytes 63971400 | solution.py:48
  344.5 7.4 %fusion.2 = (f32[512,2,8]{0,2,1:T(8,128)S(1)}, f32[2,512,512,8]{2,1,3,0:T(8,128)}) fusion(pred[512,512]{0,1:T(8,128)(4,1)S(1)} %broadcast_compare_fusion, bf16[512,2,128,1]{0,2,3,1:T(8,128)(2,1)S(1)} %bitcast.77, bf16[512,2,8,128]{3,0,2,1:T(8,128)(2,1)S(1)} %get-tuple-element.379), kind=kOutput, calls=%fused_computation.4 | convolution fusion | flops 1086316544 | bytes 19431424 | tf_op jit(solution)/shard_map/while/body/eval_jaxpr/cond/branch_1_fun/rkgd,nkd->rkgn/dot_general | solution.py:27
  351.9 9.2 %fusion.1 = f32[512,2,8]{0,2,1:T(8,128)S(1)} fusion(f32[2,512,512,8]{2,1,3,0:T(8,128)} %get-tuple-element.494, f32[512,2,8]{0,2,1:T(8,128)S(1)} %max.11, pred[512,512]{0,1:T(8,128)(4,1)S(1)} %broadcast_compare_fusion), kind=kLoop, calls=%fused_computation.3 | loop fusion | flops 16769024 | bytes 17104896 | tf_op jit(solution)/shard_map/while/body/eval_jaxpr/cond/branch_1_fun/reduce_sum | solution.py:34
  361.2 10.9 %bitcast_add_fusion = f32[512,2,8,128]{3,0,2,1:T(8,128)} fusion(f32[512,2,8,128]{3,0,2,1:T(8,128)} %get-tuple-element.381, bf16[512,2,128,1]{0,2,3,1:T(8,128)(2,1)S(1)} %bitcast.82, f32[2,512,512,8]{2,1,3,0:T(8,128)} %get-tuple-element.494, f32[512,2,8]{0,2,1:T(8,128)S(1)} %max.11, pred[512,512]{0,1:T(8,128)(4,1)S(1)} %broadcast_compare_fusion, ...), kind=kOutput, calls=%fused_computation.7 | convolution fusion | flops 1092616192 | bytes 25755648 | tf_op jit(solution)/shard_map/while/body/eval_jaxpr/cond/branch_1_fun/rkgn,nkd->rkgd/dot_general | solution.py:35
  372.1 2.9 divide_convert_fusion
  375.0 1.4 copy.19
  376.3 1.9 copy.40
  (157 shorter events, 37.8 us)
Async XLA Ops:
  7.2 32.0 %all-gather.4.cloned.1.call-start = ((), (), s32[]{:S(2)}) async-start(), calls=%async_computation.1 | async-start | bytes 2359296 | tf_op jit(solution)/shard_map/all_gather | solution.py:90
  9.0 60.3 %all-gather.6.cloned.1.call-start = ((), (), s32[]{:S(2)}) async-start(), calls=%async_computation.2 | async-start | bytes 2359296 | tf_op jit(solution)/shard_map/all_gather | solution.py:91
  10.9 105.9 %all-gather.8.cloned.1.call-start = ((), (), s32[]{:S(2)}) async-start(), calls=%async_computation.3 | async-start | bytes 1769472 | tf_op jit(solution)/shard_map/all_gather | solution.py:119
  92.2 30.0 %copy-start = (bf16[512,2048]{1,0:T(8,128)(2,1)S(1)}, bf16[512,2048]{1,0:T(8,128)(2,1)}, u32[]{:S(2)}) copy-start(bf16[512,2048]{1,0:T(8,128)(2,1)} %param.12) | copy-start | bytes 6291460
  92.3 285.9 %reduce-scatter.2.cloned.1.call-start = ((), (), s32[]{:S(2)}) async-start(), calls=%async_computation.4 | async-start | bytes 983040 | tf_op jit(solution)/shard_map/reduce_scatter | solution.py:120
Sparse Core Ops, SparseCore 0:
  10.1 28.9 all-gather.3
  40.8 28.5 all-gather.5
  92.4 24.3 all-gather.7
  122.3 26.4 reduce-scatter.1
where the time goes:
time: 386 us; the launch traced here: 385 us
  matrix products  160 us (41%)
  other arithmetic  83.5 us (22%)
  waiting for transfers between devices  81.1 us (21%)
  local copies, waits for them, and re-layouts  39.8 us (10%)
  between operations  13.9 us (4%)
  loops' own time  6.23 us (2%)
    dot_general x16, matrix products, attend(): jnp.einsum('rkgn,nkd->rkgd', powers.astype(jnp.bfloat16), expanded_value_...  91.7 us
    reduce_sum x16, other arithmetic, attend(): totals = totals * factor + jnp.sum(powers, axis=3)  77.7 us
    dot_general x16, matrix products, attend(): jnp.einsum('rkgd,nkd->rkgn', queries, expanded_key_heads, preferred_eleme...  62.8 us
    all_gather x1, waiting for transfers between devices, local(): lax.all_gather(prompt_value_rows, ('ctx', 'grp'), axis=0, tiled=True)  30.2 us
    all_gather x1, waiting for transfers between devices, local(): lax.all_gather(rotated_prompt_keys, ('ctx', 'grp'), axis=0, tiled=True)  26.4 us
    all_gather x1, waiting for transfers between devices, local(): lax.all_gather(continuation_context, ('ctx', 'grp'), axis=0, tiled=True)  24.5 us
    dynamic_slice x16, local copies, waits for them, and re-layouts, visit(): lax.dynamic_slice_in_dim(value_all, first_row, block_rows, 0)  17.1 us
    unnamed x9, local copies, waits for them, and re-layouts  9.88 us
  transfers between devices with their start and end apart: 4, of which 3 were waited for; matrix products, arithmetic and copies ran while one was open for 66% of the time, Pallas kernels for 0%

commit v1 on v0

v1 whole, which is shorter than its diff:
```python
import functools
import math

import jax
import jax.numpy as jnp
from jax import lax
from jax.experimental import pallas as pl
from jax.experimental.pallas import tpu as pltpu
from jax.sharding import PartitionSpec as P

QUERY_HEADS = 64
KEY_VALUE_HEADS = 8
HEAD_WIDTH = 128
GROUP = QUERY_HEADS // KEY_VALUE_HEADS

NEG = -1e30
SCALE = HEAD_WIDTH ** -0.5 * math.log2(math.e)
VMEM_BYTES = 60 * 1024 * 1024


def split_scaled(rows):
    scaled = rows.astype(jnp.float32) * SCALE
    high = scaled.astype(jnp.bfloat16)
    low = (scaled - high.astype(jnp.float32)).astype(jnp.bfloat16)
    return high, low


def score_tile(keys, queries):
    return lax.dot_general(
        jnp.concatenate([keys, keys], axis=1),
        queries,
        (((1,), (1,)), ((), ())),
        preferred_element_type=jnp.float32,
    )


def fold_tile(scores, values, acc_ref, unit, maxima, totals):
    raised = jnp.maximum(maxima, jnp.max(scores, axis=0, keepdims=True))
    powers = jnp.exp2(scores - raised)
    factor = jnp.exp2(maxima - raised)
    totals = totals * factor + jnp.sum(powers, axis=0, keepdims=True)
    acc_ref[unit] = acc_ref[unit] * factor + jnp.dot(
        values, powers.astype(jnp.bfloat16), preferred_element_type=jnp.float32
    )
    return raised, totals


def fold_units(score_of, values_of, acc_ref, state):
    result = []
    scores = score_of(0)
    for unit, (maxima, totals) in enumerate(state):
        following = score_of(unit + 1) if unit + 1 < len(state) else None
        result.append(fold_tile(scores, values_of(unit), acc_ref, unit, maxima, totals))
        scores = following
    return tuple(result)


def fresh(units, width):
    return tuple(
        (jnp.full((1, width), NEG, jnp.float32), jnp.zeros((1, width), jnp.float32))
        for _ in range(units)
    )


def prompt_kernel(index_ref, q_ref, k_ref, v_ref, o_ref, acc_ref, split_ref):
    rows = q_ref.shape[0]
    units = split_ref.shape[0]
    width = HEAD_WIDTH
    last = index_ref[0]
    acc_ref[...] = jnp.zeros_like(acc_ref)
    for unit in range(units):
        high, low = split_scaled(q_ref[:, unit * width : (unit + 1) * width])
        split_ref[unit, :, :width] = high
        split_ref[unit, :, width:] = low

    def block(number, state, diagonal):
        keys = k_ref[pl.ds(pl.multiple_of(number * rows, rows), rows), :]
        values = v_ref[number]

        def score_of(unit):
            scores = score_tile(keys, split_ref[unit])
            if diagonal:
                key_at = lax.broadcasted_iota(jnp.int32, scores.shape, 0)
                row_at = lax.broadcasted_iota(jnp.int32, scores.shape, 1)
                scores = jnp.where(key_at <= row_at, scores, NEG)
            return scores

        return fold_units(score_of, lambda unit: values, acc_ref, state)

    state = lax.fori_loop(
        0, last, lambda number, s: block(number, s, False), fresh(units, rows)
    )
    state = block(last, state, True)
    for unit in range(units):
        o_ref[:, unit * width : (unit + 1) * width] = (
            (acc_ref[unit] / state[unit][1]).T.astype(o_ref.dtype)
        )


def prompt_attention(my_index, queries, keys, values):
    rows, columns = queries.shape
    units = GROUP
    blocks = values.shape[0]
    scores = rows * keys.shape[0] * columns // HEAD_WIDTH
    return pl.pallas_call(
        prompt_kernel,
        out_shape=jax.ShapeDtypeStruct(queries.shape, queries.dtype),
        grid_spec=pltpu.PrefetchScalarGridSpec(
            num_scalar_prefetch=1,
            grid=(columns // (units * HEAD_WIDTH),),
            in_specs=[
                pl.BlockSpec((rows, units * HEAD_WIDTH), lambda g, i: (0, g)),
                pl.BlockSpec((keys.shape[0], HEAD_WIDTH), lambda g, i: (0, g)),
                pl.BlockSpec((blocks, HEAD_WIDTH, rows), lambda g, i: (0, g, 0)),
            ],
            out_specs=pl.BlockSpec((rows, units * HEAD_WIDTH), lambda g, i: (0, g)),
            scratch_shapes=[
                pltpu.VMEM((units, HEAD_WIDTH, rows), jnp.float32),
                pltpu.VMEM((units, rows, 2 * HEAD_WIDTH), jnp.bfloat16),
            ],
        ),
        compiler_params=pltpu.CompilerParams(vmem_limit_bytes=VMEM_BYTES),
        cost_estimate=pl.CostEstimate(
            flops=4 * scores * HEAD_WIDTH, bytes_accessed=8 * queries.size, transcendentals=scores
        ),
    )(my_index, queries, keys, values)


def decode_kernel(q_ref, k_ref, v_ref, len_ref, o_ref, acc_ref, split_ref):
    rows = q_ref.shape[0]
    units = split_ref.shape[0]
    blocks, _, block_rows = v_ref.shape
    width = HEAD_WIDTH
    acc_ref[...] = jnp.zeros_like(acc_ref)
    for unit in range(units):
        for member in range(GROUP):
            head = unit * GROUP + member
            high, low = split_scaled(q_ref[:, head * width : (head + 1) * width])
            split_ref[unit, member * rows : (member + 1) * rows, :width] = high
            split_ref[unit, member * rows : (member + 1) * rows, width:] = low
    lengths = len_ref[...]

    def block(number, state):
        first = pl.multiple_of(number * block_rows, block_rows)

        def score_of(unit):
            keys = k_ref[pl.ds(first, block_rows), unit * width : (unit + 1) * width]
            scores = score_tile(keys, split_ref[unit])
            key_at = lax.broadcasted_iota(jnp.int32, scores.shape, 0)
            return jnp.where(key_at < lengths - first, scores, NEG)

        def values_of(unit):
            return v_ref[number, unit * width : (unit + 1) * width, :]

        return fold_units(score_of, values_of, acc_ref, state)

    state = lax.fori_loop(0, blocks, block, fresh(units, rows * GROUP))
    for unit in range(units):
        context = (acc_ref[unit] / state[unit][1]).T.astype(o_ref.dtype)
        for member in range(GROUP):
            head = unit * GROUP + member
            o_ref[:, head * width : (head + 1) * width] = context[
                member * rows : (member + 1) * rows
            ]


def decode_attention(queries, keys, values, lengths):
    rows, columns = queries.shape
    units = columns // (GROUP * HEAD_WIDTH)
    lanes = jnp.tile(lengths, GROUP)[None, :]
    scores = rows * keys.shape[0] * columns // HEAD_WIDTH
    return pl.pallas_call(
        decode_kernel,
        out_shape=jax.ShapeDtypeStruct(queries.shape, queries.dtype),
        scratch_shapes=[
            pltpu.VMEM((units, HEAD_WIDTH, rows * GROUP), jnp.float32),
            pltpu.VMEM((units, rows * GROUP, 2 * HEAD_WIDTH), jnp.bfloat16),
        ],
        compiler_params=pltpu.CompilerParams(vmem_limit_bytes=VMEM_BYTES),
        cost_estimate=pl.CostEstimate(
            flops=4 * scores * HEAD_WIDTH, bytes_accessed=4 * keys.size, transcendentals=scores
        ),
    )(queries, keys, values, lanes)


def local(
    prompt_queries,
    rotated_prompt_keys,
    prompt_value_rows,
    continuation_queries,
    prefix_len,
    out_weight,
):
    along = ("ctx", "grp")
    my_index = lax.axis_index(along)
    keys = lax.all_gather(rotated_prompt_keys, along, axis=0, tiled=True)
    values = lax.all_gather(prompt_value_rows.T, along, axis=0)

    own_rows = continuation_queries.shape[0]
    lengths = lax.dynamic_slice_in_dim(prefix_len, my_index * own_rows, own_rows, 0)
    continuation_context = decode_attention(continuation_queries, keys, values, lengths)
    gathered = lax.all_gather(continuation_context, along, axis=0, tiled=True)
    mixed = lax.psum_scatter(
        jnp.dot(gathered, out_weight, preferred_element_type=jnp.float32).astype(jnp.bfloat16),
        "head",
        scatter_dimension=0,
        tiled=True,
    )
    prompt_context = prompt_attention(my_index[None].astype(jnp.int32), prompt_queries, keys, values)
    return (prompt_context, mixed)


def solution(mesh):
    in_specs = (
        P(("ctx", "grp"), "head"),
        P(("ctx", "grp"), "head"),
        P(("ctx", "grp"), "head"),
        P(("ctx", "grp"), "head"),
        P(),
        P("head", ("ctx", "grp")),
    )
    out_specs = (P(("ctx", "grp"), "head"), P("head", ("ctx", "grp")))
    return jax.shard_map(local, mesh=mesh, in_specs=in_specs, out_specs=out_specs, check_vma=False)
```

time: 386 us -> 168 us (0.44)
  matrix products: 160 us -> 5.34 us
  other arithmetic: 83.5 us -> 0 us
  Pallas kernels: 0 us -> 61.2 us
  local copies, waits for them, and re-layouts: 39.8 us -> 5.32 us
  loops' own time: 6.23 us -> 0 us
    dot_general x32 -> x0, matrix products: 155 us -> none  [the longest x16 91.7 us: attend(): jnp.einsum('rkgn,nkd->rkgd', powers.astype(jnp.bfloat16), expanded_value_...]
    reduce_sum x16 -> x0, other arithmetic: 77.7 us -> none  [attend(): totals = totals * factor + jnp.sum(powers, axis=3)]
    pallas_call x0 -> x2, Pallas kernels: none -> 61.2 us  [the longest x1 51.2 us: prompt_attention(): pl.pallas_call(prompt_kernel, out_shape=jax.ShapeDtypeStruct(queries.shap...]
    dynamic_slice x16 -> x0, local copies, waits for them, and re-layouts: 17.1 us -> none  [visit(): lax.dynamic_slice_in_dim(value_all, first_row, block_rows, 0)]
    unnamed x9 -> x0, local copies, waits for them, and re-layouts: 9.88 us -> none
    another operation x10 -> x0, loops' own time: 6.23 us -> none  [the longest x2 5.71 us: local_fold(): return lax.fori_loop(0, block_count, visit, initial)]
    slice x8 -> x0, local copies, waits for them, and re-layouts: 5.05 us -> none  [prompt_step(): places[-1]]
    all_gather x0 -> x1, local copies, waits for them, and re-layouts: none -> 3.91 us  [local(): values = lax.all_gather(prompt_value_rows.T, along, axis=0)]
  transfers between devices with their start and end apart: 4 -> 4, of which waited for: 3 -> 3; matrix products, arithmetic and copies ran while one was open for 66% -> 3% of each run, Pallas kernels for 0% -> 31%
where the time goes in v1:
time: 168 us; the launch traced here: 167 us
  waiting for transfers between devices  81.7 us (49%)
  Pallas kernels  61.2 us (36%)
  between operations  13.8 us (8%)
  matrix products  5.34 us (3%)
  local copies, waits for them, and re-layouts  5.32 us (3%)
    pallas_call x1, Pallas kernels, prompt_attention(): pl.pallas_call(prompt_kernel, out_shape=jax.ShapeDtypeStruct(queries.shap...  51.2 us
    all_gather x1, waiting for transfers between devices, local(): values = lax.all_gather(prompt_value_rows.T, along, axis=0)  29.2 us
    all_gather x1, waiting for transfers between devices, local(): keys = lax.all_gather(rotated_prompt_keys, along, axis=0, tiled=True)  26.6 us
    all_gather x1, waiting for transfers between devices, local(): gathered = lax.all_gather(continuation_context, along, axis=0, tiled=True)  24.5 us
    pallas_call x1, Pallas kernels, decode_attention(): pl.pallas_call(decode_kernel, out_shape=jax.ShapeDtypeStruct(queries.shap...  9.97 us
    dot_general x1, matrix products, local(): jnp.dot(gathered, out_weight, preferred_element_type=jnp.float32)  5.34 us
    all_gather x1, local copies, waits for them, and re-layouts, local(): values = lax.all_gather(prompt_value_rows.T, along, axis=0)  3.91 us
  transfers between devices with their start and end apart: 4, of which 3 were waited for; matrix products, arithmetic and copies ran while one was open for 3% of the time, Pallas kernels for 31%

profile of v1, /device:TPU:25, one launch (start us, length us, event | category | flops | bytes accessed | tf_op | source)
XLA Modules:
  0.0 167.5 jit_solution(17034867166872397446)
XLA Ops:
  7.2 0.0 all-gather.9.cloned.1.call-start
  7.2 0.7 all-gather.9.cloned.1.call-update
  7.9 0.0 all-gather.5.cloned.1.call-start
  7.9 0.7 all-gather.5.cloned.1.call-update
  8.6 0.0 all-gather.7.cloned.1.call-start
  8.7 0.8 dynamic_slice.3
  9.5 0.6 broadcast_in_dim_tile.3.len_ref
  10.1 29.2 %all-gather.9.cloned.1.call-done = bf16[2048,512]{0,1:T(8,128)(2,1)} async-done(((bf16[256,512]{0,1:T(8,128)(2,1)}), bf16[2048,512]{0,1:T(8,128)(2,1)}) %all-gather.9.cloned.1.call-update) | async-done | bytes 2097168 | tf_op jit(solution)/shard_map/all_gather | solution.py:197
  39.3 3.9 %copy.8 = bf16[2048,512]{1,0:T(8,128)(2,1)} copy(bf16[2048,512]{0,1:T(8,128)(2,1)} %all-gather.9.cloned.1.call-done) | data formatting | bytes 4194304 | tf_op jit(solution)/shard_map/all_gather | solution.py:197
  43.2 26.6 %all-gather.5.cloned.1.call-done.k_ref = bf16[4096,256]{1,0:T(8,128)(2,1)} async-done(((bf16[512,256]{1,0:T(8,128)(2,1)}), bf16[4096,256]{1,0:T(8,128)(2,1)}) %all-gather.5.cloned.1.call-update) | async-done | bytes 2097168 | tf_op jit(solution)/shard_map/all_gather | solution.py:196
  69.9 10.0 %shard_map.78 = bf16[48,2048]{1,0:T(8,128)(2,1)} custom-call(bf16[48,2048]{1,0:T(8,128)(2,1)} %q_ref.3, bf16[4096,256]{1,0:T(8,128)(2,1)} %all-gather.5.cloned.1.call-done.k_ref, bf16[8,256,512]{2,1,0:T(8,128)(2,1)} %bitcast.5, s32[1,384]{1,0:T(1,128)} %broadcast_in_dim_tile.3.len_ref), custom_call_target="tpu_custom_call" | custom-call | flops 1610612736 | bytes 4194304 | tf_op jit(solution)/shard_map/pallas_call | solution.py:172
  79.8 0.0 all-gather.7.cloned.1.call-update
  79.9 0.0 reduce-scatter.2.cloned.1.call-start
  79.9 24.5 %all-gather.7.cloned.1.call-done = bf16[384,2048]{1,0:T(8,128)(2,1)} async-done(((bf16[48,2048]{1,0:T(8,128)(2,1)}), bf16[384,2048]{1,0:T(8,128)(2,1)}) %all-gather.7.cloned.1.call-update) | async-done | bytes 1572880 | tf_op jit(solution)/shard_map/all_gather | solution.py:202
  104.4 5.3 %convolution_convert_fusion = bf16[384,1024]{1,0:T(8,128)(2,1)} fusion(bf16[384,2048]{1,0:T(8,128)(2,1)} %all-gather.7.cloned.1.call-done, bf16[2048,1024]{1,0:T(8,128)(2,1)} %param.11), kind=kOutput, calls=%fused_computation | convolution fusion | flops 1611005952 | bytes 6553600 | tf_op jit(solution)/shard_map/dot_general | solution.py:204
  109.7 0.0 reduce-scatter.2.cloned.1.call-update
  109.8 51.2 %shard_map.77 = bf16[512,2048]{1,0:T(8,128)(2,1)} custom-call(s32[1]{0:T(128)} %bitcast.index_ref, bf16[512,2048]{1,0:T(8,128)(2,1)} %q_ref.2, bf16[4096,256]{1,0:T(8,128)(2,1)} %all-gather.5.cloned.1.call-done.k_ref, bf16[8,256,512]{2,1,0:T(8,128)(2,1)} %bitcast.6), custom_call_target="tpu_custom_call" | custom-call | flops 17179869184 | bytes 8388608 | tf_op jit(solution)/shard_map/pallas_call | solution.py:105
  160.9 0.0 reduce-scatter.2.cloned.1.call-done
  (1 shorter events, 0.0 us)
Async XLA Ops:
  7.2 32.2 %all-gather.9.cloned.1.call-start = ((), (), s32[]{:S(2)}) async-start(), calls=%async_computation.4 | async-start | bytes 2359296 | tf_op jit(solution)/shard_map/all_gather | solution.py:197
  7.9 62.0 %all-gather.5.cloned.1.call-start = ((), (), s32[]{:S(2)}) async-start(), calls=%async_computation.1 | async-start | bytes 2359296 | tf_op jit(solution)/shard_map/all_gather | solution.py:196
  8.6 95.7 %all-gather.7.cloned.1.call-start = ((), (), s32[]{:S(2)}) async-start(), calls=%async_computation.2 | async-start | bytes 1769472 | tf_op jit(solution)/shard_map/all_gather | solution.py:202
  79.9 81.1 %reduce-scatter.2.cloned.1.call-start = ((), (), s32[]{:S(2)}) async-start(), calls=%async_computation.3 | async-start | bytes 983040 | tf_op jit(solution)/shard_map/reduce_scatter | solution.py:203
Sparse Core Ops, SparseCore 0:
  9.6 29.7 all-gather.8
  40.9 28.8 all-gather.4
  80.0 24.3 all-gather.6
  109.9 26.4 reduce-scatter.1
